TPU v7x, 32 devices: a whole 2x2x4 slice. The times are simulated.
32 devices in a mesh: leaf: 8 (over z, y), blk: 4 (over x, core).
Axes of the slice: x: 2, y: 2, z: 4, core: 2. Of those that a mesh axis runs over, the one named last changes fastest.
Arguments:
- src_pos: int32 [4, 2097152], P('blk', 'leaf'), may hold values from 0 to 8388607, as said below
- strengths: float32 [2, 4, 2097152], P(None, 'blk', 'leaf'), may hold values from -0.001953125 to 0.001953125
- tgt_pos: int32 [8388608], P(('leaf', 'blk')), may hold values from 0 to 201326591, as said below
Outputs:
- field: float32 [2, 8388608], P(None, ('leaf', 'blk'))
Inputs may be any that keep to these rules, and one draw needn't show every extreme that they name: `src_pos`: row q holds 16384 runs of 128 cells; run b lies in the 128 cells from (q * 16384 + b) * 128 on. `tgt_pos`: the ticks held by index k of leaf, at every index of blk, come in 2048 runs of 128; run j lies in the 12288 ticks from (j * 8 + r) * 12288 on, where r is k with its 3 binary digits in reverse order.
All inputs are finite; a program needn't handle non-finite values.
Results may differ from a plain program's by a relative error of at most 0.0003.
Values sent between devices are 32-bit elements; how exact they have to be, the bound alone decides.
A program may use at most 128 MiB of HBM per device.

v0:
```python
import functools
import math

import jax
import jax.numpy as jnp
import numpy as np
from jax import lax
from jax.experimental import pallas as pl
from jax.experimental.pallas import tpu as pltpu
from jax.sharding import PartitionSpec as P

R = 16
PER_BOX = 128
TGT_BOX = 128
BOX_CELLS = 128
TOP_TICKS = 201326592
LANES = 128
HIGHEST = lax.Precision.HIGHEST


def fit_even(values, span, count):
    u = 0.5 * span * span * (1.0 + np.cos(np.pi * (np.arange(400) + 0.5) / 400))
    cheb = np.polynomial.chebyshev.Chebyshev.fit(u, values(np.sqrt(u)), count - 1, domain=[0, span * span])
    return [float(c) for c in cheb.convert(kind=np.polynomial.Polynomial).coef]


COS_POLY = fit_even(lambda y: np.cos(2 * np.pi * y), 0.5, 6)
SIN_POLY = fit_even(lambda y: np.sin(2 * np.pi * y) / y, 0.5, 6)


def horner(coefs, u):
    out = u * coefs[-1] + coefs[-2]
    for c in coefs[-3::-1]:
        out = out * u + c
    return out


def cos_sin_turns(y):
    u = y * y
    return horner(COS_POLY, u), y * horner(SIN_POLY, u)


def node_offsets(box_cells):
    node_index = np.arange(R)
    unit_nodes = (1.0 - np.cos(np.pi * (node_index + 0.5) / R)) / 2.0
    return np.floor(box_cells * unit_nodes).astype(np.int64)


def lagrange_values(node_pos, points):
    rows = []
    for row_node in range(node_pos.shape[0]):
        column = np.ones(points.shape[0])
        for other in range(node_pos.shape[0]):
            if other != row_node:
                column = column * (points - node_pos[other]) / (node_pos[row_node] - node_pos[other])
        rows.append(column)
    return np.stack(rows)


def as_real(m):
    return np.block([[m.real, -m.imag], [m.imag, m.real]])


def turn64(a, b):
    product = (a * b + 2**31) % 2**32 - 2**31
    return product * (2.0 * np.pi / 2.0**32)


@functools.cache
def step_matrix(level):
    cells = BOX_CELLS * 2**level
    child, parent = node_offsets(cells), node_offsets(2 * cells)
    inner = np.concatenate([child, child + cells])
    blend = lagrange_values(parent / (2.0 * cells), inner / (2.0 * cells)).reshape(R, 2, R)
    half = TOP_TICKS // 2 ** (level + 2)
    assert half * cells % 2**32 == 2**31
    out = np.zeros((2, 2, 2 * R, 2 * R))
    for e in range(2):
        phase = np.exp(1j * turn64(half if e else -half, child))
        for j in range(2):
            out[e, j] = as_real((-1.0) ** j * blend[:, j, :] * phase[None, :])
    return out


def radix_matrix(first, count):
    total = np.eye(2 * R)[None, None]
    for k in range(count):
        m = step_matrix(first + k)
        n = total.shape[0]
        new = np.zeros((2 * n, 2 * n, 2 * R, 2 * R))
        for a in range(n):
            for b in range(n):
                for e in range(2):
                    for j in range(2):
                        new[2 * a + e, b + j * n] = m[e, j] @ total[a, b]
        total = new
    n = total.shape[0]
    return total.transpose(0, 2, 1, 3).reshape(n * 2 * R, n * 2 * R)


def fold_pairs():
    eye = np.eye(R)
    plus = eye[: R // 2] + eye[::-1][: R // 2]
    minus = eye[: R // 2] - eye[::-1][: R // 2]
    zero = np.zeros_like(plus)
    return np.block([[plus, zero], [zero, plus], [zero, -minus], [minus, zero]])


def leaf_matrix():
    nodes = node_offsets(BOX_CELLS)
    angles = np.pi * (np.arange(R) + 0.5) / R
    at_exact = lagrange_values(2.0 * nodes / BOX_CELLS - 1.0, np.cos(angles))
    cheb_at = np.stack([np.cos(n * angles) for n in range(R)])
    norm = np.where(np.arange(R) == 0, 1.0, 2.0) / R
    g = (norm[:, None] * (cheb_at @ at_exact.T)).astype(np.float32)
    wide = np.repeat(g.T, 8, axis=1)
    zero = np.zeros_like(wide)
    return np.block([[wide, zero], [zero, wide]]).astype(np.float32)


def leaf_kernel(pos_ref, str_ref, mix_ref, out_ref, p_t, re_t, im_t, *, digits):
    beta = pl.program_id(0)
    rows = pl.ds(beta, LANES, stride=digits)
    p_t[...] = pos_ref[rows, :].T
    re_t[...] = str_ref[0, rows, :].T
    im_t[...] = str_ref[1, rows, :].T

    def chunk(i, acc):
        here = pl.ds(pl.multiple_of(i * 8, 8), 8)
        r = p_t[here, :] & (BOX_CELLS - 1)
        turn = (r * (TOP_TICKS // 2)).astype(jnp.float32) * (2.0**-32)
        c, s = cos_sin_turns(turn)
        a, b = re_t[here, :], im_t[here, :]
        v = r.astype(jnp.float32) * (2.0 / BOX_CELLS) - 1.0
        v2 = v + v
        re0, im0 = c * a - s * b, s * a + c * b
        re1, im1 = v * re0, v * im0
        new = [(re0, im0), (re1, im1)]
        for _ in range(2, R):
            re0, re1 = re1, v2 * re1 - re0
            im0, im1 = im1, v2 * im1 - im0
            new.append((re1, im1))
        return tuple((x + u, y + w) for (x, y), (u, w) in zip(acc, new))

    zero = jnp.zeros((8, LANES), jnp.float32)
    acc = lax.fori_loop(0, PER_BOX // 8, chunk, tuple((zero, zero) for _ in range(R)), unroll=2)
    stack = jnp.concatenate([x for x, _ in acc] + [y for _, y in acc], axis=0)
    out_ref[0] = jnp.dot(mix_ref[...], stack, precision=HIGHEST, preferred_element_type=jnp.float32)


def leaf_call(pos, strengths):
    boxes = pos.shape[0]
    digits = boxes // LANES
    whole = pl.BlockSpec(memory_space=pltpu.VMEM)
    return pl.pallas_call(
        functools.partial(leaf_kernel, digits=digits),
        grid=(digits,),
        out_shape=jax.ShapeDtypeStruct((digits, 2 * R, LANES), jnp.float32),
        in_specs=[whole, whole, whole],
        out_specs=pl.BlockSpec((1, 2 * R, LANES), lambda b: (b, 0, 0)),
        scratch_shapes=[
            pltpu.VMEM((LANES, LANES), jnp.int32),
            pltpu.VMEM((LANES, LANES), jnp.float32),
            pltpu.VMEM((LANES, LANES), jnp.float32),
        ],
        name="leaf",
    )(pos, strengths, jnp.asarray(leaf_matrix()))


def eval_kernel(suffix_ref, tgt_ref, co_ref, out_ref, g_t, re_t, im_t, *, blocks, leaves, depth, rows):
    cells = BOX_CELLS * 2**depth
    ticks = TOP_TICKS // 2**depth
    half = R // 2
    tile = pl.program_id(0)
    lane = lax.broadcasted_iota(jnp.int32, (1, LANES), 1)
    box = (tile * LANES + lane) * leaves + suffix_ref[0]
    center = box * ticks + ticks // 2
    g_t[...] = (tgt_ref[...].T - center).astype(jnp.float32)
    offsets = 2 * node_offsets(cells) - cells + 1

    def turned(g, factor):
        y = g * factor
        if abs(factor) * (ticks // 2) > 0.5:
            y = y - jnp.round(y)
        return cos_sin_turns(y)

    def chunk(i, carry):
        here = pl.ds(pl.multiple_of(i * rows, rows), rows)
        g = g_t[here, :]
        acc = [[None, None] for _ in range(blocks)]
        for t in range(half):
            c, s = turned(g, float(offsets[t]) * 2.0**-33)
            for q in range(blocks):
                for part in range(2):
                    sc = co_ref[q, pl.ds(part * half + t, 1), :]
                    sd = co_ref[q, pl.ds((2 + part) * half + t, 1), :]
                    term = sc * c + sd * s
                    acc[q][part] = term if t == 0 else acc[q][part] + term
        zc, zs = turned(g, float(cells) * 2.0**-32)
        re, im = acc[blocks - 1]
        for q in range(blocks - 2, -1, -1):
            re, im = zc * re - zs * im + acc[q][0], zc * im + zs * re + acc[q][1]
        pc, ps = turned(g, float(cells - 1) * 2.0**-33)
        re_t[here, :] = pc * re - ps * im
        im_t[here, :] = pc * im + ps * re
        return carry

    lax.fori_loop(0, TGT_BOX // rows, chunk, 0)
    out_ref[pl.ds(0, LANES, stride=2), :] = re_t[...].T
    out_ref[pl.ds(1, LANES, stride=2), :] = im_t[...].T


def eval_call(suffix, ticks, coefs, leaves, depth):
    boxes = ticks.shape[0]
    blocks = coefs.shape[0]
    return pl.pallas_call(
        functools.partial(eval_kernel, blocks=blocks, leaves=leaves, depth=depth, rows=16),
        grid=(boxes // LANES,),
        out_shape=jax.ShapeDtypeStruct((2 * boxes, TGT_BOX), jnp.float32),
        in_specs=[
            pl.BlockSpec(memory_space=pltpu.SMEM),
            pl.BlockSpec((LANES, TGT_BOX), lambda i: (i, 0)),
            pl.BlockSpec((blocks, 2 * R, LANES), lambda i: (0, 0, i)),
        ],
        out_specs=pl.BlockSpec((2 * LANES, TGT_BOX), lambda i: (i, 0)),
        scratch_shapes=[pltpu.VMEM((TGT_BOX, LANES), jnp.float32)] * 3,
        name="evaluate",
    )(suffix.reshape(1), ticks, coefs)


def table(m):
    return jnp.asarray(m.astype(np.float32))


def mm(a, b):
    return jnp.dot(a, b, precision=HIGHEST, preferred_element_type=jnp.float32)


def local_tree(leaf, boxes):
    low = leaf.shape[0]
    n1 = low.bit_length() - 1
    rest = boxes.bit_length() - 1 - n1
    n2 = rest - rest // 2
    n3 = rest - n2
    c = 2 * R
    y = mm(table(radix_matrix(0, n1)), leaf.reshape(low * c, -1))
    y = y.reshape(low, c, 2**n3, 2**n2).transpose(3, 1, 0, 2).reshape(2**n2 * c, -1)
    y = mm(table(radix_matrix(n1, n2)), y)
    y = y.reshape(2**n2, c, low, 2**n3).transpose(3, 1, 2, 0).reshape(2**n3 * c, -1)
    y = mm(table(radix_matrix(n1 + n2, n3)), y)
    return y.reshape(2**n3, c, low * 2**n2).transpose(1, 2, 0).reshape(c, boxes)


def local(src_pos, strengths, tgt_pos):
    leaf_count = lax.axis_size("leaf")
    leaf_bits = leaf_count.bit_length() - 1
    leaf_no = lax.axis_index("leaf")
    boxes = src_pos.shape[1] // PER_BOX
    local_depth = boxes.bit_length() - 1
    leaf = leaf_call(src_pos.reshape(boxes, PER_BOX), strengths.reshape(2, boxes, PER_BOX))
    weights = local_tree(leaf, boxes)
    suffix = jnp.int32(0)
    for bit_no in range(leaf_bits):
        side = leaf_no // 2**bit_no % 2
        route = [(k, k ^ (1 << bit_no)) for k in range(leaf_count)]
        partner = lax.ppermute(weights, "leaf", route)
        m = step_matrix(local_depth + bit_no)
        if bit_no == leaf_bits - 1:
            m = np.einsum("xy,ejyz->ejxz", fold_pairs(), m)
        own = jnp.where(side == 0, table(m[0, 0]), table(m[1, 1]))
        other = jnp.where(side == 0, table(m[0, 1]), table(m[1, 0]))
        weights = mm(own, weights) + mm(other, partner)
        suffix = 2 * suffix + side
    half = boxes // 2
    parts = [lax.all_gather(weights[None, :, i * half : (i + 1) * half], "blk", axis=0, tiled=True) for i in range(2)]
    coefs = jnp.concatenate(parts, axis=2)
    out = eval_call(suffix, tgt_pos.reshape(boxes, TGT_BOX), coefs, leaf_count, local_depth + leaf_bits)
    return out.reshape(boxes, 2, TGT_BOX).transpose(1, 0, 2).reshape(2, boxes * TGT_BOX)


def solution(mesh):
    return jax.shard_map(
        local,
        mesh=mesh,
        in_specs=(P("blk", "leaf"), P(None, "blk", "leaf"), P(("leaf", "blk"))),
        out_specs=P(None, ("leaf", "blk")),
        check_vma=False,
    )
```

profile of v0, /device:TPU:0, one launch (start us, length us, event | category | flops | bytes accessed | tf_op | source)
XLA Modules:
  0.0 94.0 jit_solution(4637274770403583390)
XLA Ops:
  0.0 15.5 %leaf.1 = f32[16,32,128]{2,1,0:T(8,128)} custom-call(s32[2048,128]{1,0:T(8,128)} %bitcast.51, f32[2,2048,128]{2,1,0:T(8,128)} %bitcast.46, f32[32,256]{1,0:T(8,128)} %constant.90.clone.mix_ref), custom_call_target="tpu_custom_call" | custom-call | tf_op jit(solution)/shard_map/leaf/pallas_call | solution.py:155
  15.5 2.1 %fusion.17 = f32[512,128]{0,1:T(8,128)S(1)} fusion(f32[512,512]{1,0:T(8,128)S(1)} %copy-done.1, f32[512,128]{1,0:T(8,128)} %bitcast.52), kind=kOutput, calls=%fused_computation.21 | convolution fusion | flops 402653184 | bytes 1572864 | tf_op jit(solution)/shard_map/dot_general | solution.py:236
  18.0 0.3 copy.28
  18.3 0.4 reshape.45
  18.9 1.2 %fusion.18 = f32[512,128]{0,1:T(8,128)S(1)} fusion(f32[512,512]{1,0:T(8,128)S(1)} %copy-done, f32[512,128]{0,1:T(8,128)S(1)} %reshape.45), kind=kOutput, calls=%fused_computation.22 | convolution fusion | flops 402653184 | bytes 1572864 | tf_op jit(solution)/shard_map/dot_general | solution.py:236
  20.4 0.3 copy.30
  21.1 0.4 fusion.19
  21.5 0.4 copy.31
  22.3 3.1 %collective-permute-start = (f32[32,2048]{1,0:T(8,128)S(1)}, f32[32,2048]{1,0:T(8,128)S(1)}, u32[]{:S(2)}, u32[]{:S(2)}) collective-permute-start(f32[32,2048]{1,0:T(8,128)S(1)} %copy.32), channel_id=1, source_target_pairs={{0,4},{4,0},{8,12},{12,8},{16,20},{20,16},{24,28},{28,24},{1,5},{5... | collective-permute-start | bytes 786440 | tf_op jit(solution)/shard_map/ppermute | solution.py:266
  25.4 1.1 %fusion.3 = f32[32,2048]{1,0:T(8,128)S(1)} fusion(f32[32,32]{1,0:T(8,128)S(1)} %copy-done.4, f32[32,32]{1,0:T(8,128)S(1)} %copy-done.3, pred[]{:T(512)S(6)} %eq.18, f32[8,32,256]{1,0,2:T(8,128)S(1)} %copy.31), kind=kOutput, calls=%fused_computation.7 | convolution fusion | flops 25166848 | bytes 532481 | tf_op jit(solution)/shard_map/dot_general | solution.py:236
  26.5 5.2 %collective-permute-done = f32[32,2048]{1,0:T(8,128)S(1)} collective-permute-done((f32[32,2048]{1,0:T(8,128)S(1)}, f32[32,2048]{1,0:T(8,128)S(1)}, u32[]{:S(2)}, u32[]{:S(2)}) %collective-permute-start) | collective-permute-done | bytes 262176 | tf_op jit(solution)/shard_map/ppermute | solution.py:266
  31.7 0.4 convolution_add_fusion.2
  32.1 1.9 %collective-permute-start.1 = (f32[32,2048]{1,0:T(8,128)S(1)}, f32[32,2048]{1,0:T(8,128)S(1)}, u32[]{:S(2)}, u32[]{:S(2)}) collective-permute-start(f32[32,2048]{1,0:T(8,128)S(1)} %convolution_add_fusion.2), channel_id=1, source_target_pairs={{0,8},{4,12},{8,0},{12,4},{16,24},{20,28},{24,16},{28,20},{1,9},{5... | collective-permute-start | bytes 786440 | tf_op jit(solution)/shard_map/ppermute | solution.py:266
  33.9 0.4 fusion.5
  34.3 5.3 %collective-permute-done.1 = f32[32,2048]{1,0:T(8,128)S(1)} collective-permute-done((f32[32,2048]{1,0:T(8,128)S(1)}, f32[32,2048]{1,0:T(8,128)S(1)}, u32[]{:S(2)}, u32[]{:S(2)}) %collective-permute-start.1) | collective-permute-done | bytes 262176 | tf_op jit(solution)/shard_map/ppermute | solution.py:266
  39.6 0.4 convolution_add_fusion.1
  40.0 2.6 %collective-permute-start.2 = (f32[32,2048]{1,0:T(8,128)S(1)}, f32[32,2048]{1,0:T(8,128)S(1)}, u32[]{:S(2)}, u32[]{:S(2)}) collective-permute-start(f32[32,2048]{1,0:T(8,128)S(1)} %convolution_add_fusion.1), channel_id=1, source_target_pairs={{0,16},{4,20},{8,24},{12,28},{16,0},{20,4},{24,8},{28,12},{1,17},{... | collective-permute-start | bytes 786440 | tf_op jit(solution)/shard_map/ppermute | solution.py:266
  42.6 0.3 fusion.7
  42.9 10.2 %collective-permute-done.2 = f32[32,2048]{1,0:T(8,128)S(1)} collective-permute-done((f32[32,2048]{1,0:T(8,128)S(1)}, f32[32,2048]{1,0:T(8,128)S(1)}, u32[]{:S(2)}, u32[]{:S(2)}) %collective-permute-start.2) | collective-permute-done | bytes 262176 | tf_op jit(solution)/shard_map/ppermute | solution.py:266
  53.2 0.4 convolution_add_fusion
  53.6 6.8 %all-gather = f32[128,1024]{1,0:T(8,128)S(1)} all-gather(f32[32,1024]{1,0:T(8,128)S(1)} %get-tuple-element.5), channel_id=2, replica_groups=mesh['leaf'=8,'blk'=4] {'blk'}, dimensions={0}, use_global_device_ids=true | all-gather | bytes 655360 | tf_op jit(solution)/shard_map/all_gather | solution.py:275
  60.4 7.3 %all-gather.1 = f32[128,1024]{1,0:T(8,128)S(1)} all-gather(f32[32,1024]{1,0:T(8,128)S(1)} %get-tuple-element.6), channel_id=3, replica_groups=mesh['leaf'=8,'blk'=4] {'blk'}, dimensions={0}, use_global_device_ids=true | all-gather | bytes 655360 | tf_op jit(solution)/shard_map/all_gather | solution.py:275
  67.7 1.1 %pad_maximum_fusion.co_ref = f32[4,32,2048]{2,1,0:T(8,128)} fusion(f32[4,32,1024]{2,1,0:T(8,128)S(1)} %bitcast.48, f32[4,32,1024]{2,1,0:T(8,128)S(1)} %bitcast.47), kind=kLoop, calls=%fused_computation.3 | loop fusion | flops 262144 | bytes 2097152 | tf_op jit(solution)/shard_map/concatenate | solution.py:276
  68.7 25.2 %evaluate.1 = f32[4096,128]{1,0:T(8,128)} custom-call(s32[1]{0:T(128)} %bitcast.suffix_ref, s32[2048,128]{1,0:T(8,128)} %bitcast.49, f32[4,32,2048]{2,1,0:T(8,128)} %pad_maximum_fusion.co_ref), custom_call_target="tpu_custom_call" | custom-call | tf_op jit(solution)/shard_map/evaluate/pallas_call | solution.py:216
  (35 shorter events, 1.4 us)
Async XLA Ops:
  0.0 15.5 %copy-start.1 = (f32[512,512]{1,0:T(8,128)S(1)}, f32[512,512]{1,0:T(8,128)}, u32[]{:S(2)}) copy-start(f32[512,512]{1,0:T(8,128)} %constant.91.clone) | copy-start | bytes 3145732
  17.7 1.2 %copy-start = (f32[512,512]{1,0:T(8,128)S(1)}, f32[512,512]{1,0:T(8,128)}, u32[]{:S(2)}) copy-start(f32[512,512]{1,0:T(8,128)} %constant.92.clone) | copy-start | bytes 3145732
  20.1 1.0 %copy-start.2 = (f32[256,256]{1,0:T(8,128)S(1)}, f32[256,256]{1,0:T(8,128)}, u32[]{:S(2)}) copy-start(f32[256,256]{1,0:T(8,128)} %constant.93.clone) | copy-start | bytes 786436
  20.8 4.7 %copy-start.3 = (f32[32,32]{1,0:T(8,128)S(1)}, f32[32,32]{1,0:T(8,128)}, u32[]{:S(2)}) copy-start(f32[32,32]{1,0:T(8,128)} %constant.95.clone) | copy-start | bytes 12292
  20.8 4.6 %copy-start.4 = (f32[32,32]{1,0:T(8,128)S(1)}, f32[32,32]{1,0:T(8,128)}, u32[]{:S(2)}) copy-start(f32[32,32]{1,0:T(8,128)} %constant.94.clone) | copy-start | bytes 12292
  21.5 10.2 %copy-start.13 = (f32[32,32]{1,0:T(8,128)S(1)}, f32[32,32]{1,0:T(8,128)}, u32[]{:S(2)}) copy-start(f32[32,32]{1,0:T(8,128)} %constant.97.clone) | copy-start | bytes 12292
  21.5 10.2 %copy-start.14 = (f32[32,32]{1,0:T(8,128)S(1)}, f32[32,32]{1,0:T(8,128)}, u32[]{:S(2)}) copy-start(f32[32,32]{1,0:T(8,128)} %constant.96.clone) | copy-start | bytes 12292
  22.0 12.0 %copy-start.11 = (f32[32,32]{1,0:T(8,128)S(1)}, f32[32,32]{1,0:T(8,128)}, u32[]{:S(2)}) copy-start(f32[32,32]{1,0:T(8,128)} %constant.99.clone) | copy-start | bytes 12292
  22.0 12.0 %copy-start.12 = (f32[32,32]{1,0:T(8,128)S(1)}, f32[32,32]{1,0:T(8,128)}, u32[]{:S(2)}) copy-start(f32[32,32]{1,0:T(8,128)} %constant.98.clone) | copy-start | bytes 12292
  22.0 17.6 %copy-start.9 = (f32[32,32]{1,0:T(8,128)S(1)}, f32[32,32]{1,0:T(8,128)}, u32[]{:S(2)}) copy-start(f32[32,32]{1,0:T(8,128)} %constant.101.clone) | copy-start | bytes 12292
  22.0 17.6 %copy-start.10 = (f32[32,32]{1,0:T(8,128)S(1)}, f32[32,32]{1,0:T(8,128)}, u32[]{:S(2)}) copy-start(f32[32,32]{1,0:T(8,128)} %constant.100.clone) | copy-start | bytes 12292
  22.3 20.3 %copy-start.7 = (f32[32,32]{1,0:T(8,128)S(1)}, f32[32,32]{1,0:T(8,128)}, u32[]{:S(2)}) copy-start(f32[32,32]{1,0:T(8,128)} %constant.103.clone) | copy-start | bytes 12292
  22.3 20.3 %copy-start.8 = (f32[32,32]{1,0:T(8,128)S(1)}, f32[32,32]{1,0:T(8,128)}, u32[]{:S(2)}) copy-start(f32[32,32]{1,0:T(8,128)} %constant.102.clone) | copy-start | bytes 12292
  22.3 9.4 %collective-permute-start = (f32[32,2048]{1,0:T(8,128)S(1)}, f32[32,2048]{1,0:T(8,128)S(1)}, u32[]{:S(2)}, u32[]{:S(2)}) collective-permute-start(f32[32,2048]{1,0:T(8,128)S(1)} %copy.32), channel_id=1, source_target_pairs={{0,4},{4,0},{8,12},{12,8},{16,20},{20,16},{24,28},{28,24},{1,5},{5... | collective-permute-start | bytes 786440 | tf_op jit(solution)/shard_map/ppermute | solution.py:266
  25.4 27.8 %copy-start.5 = (f32[32,32]{1,0:T(8,128)S(1)}, f32[32,32]{1,0:T(8,128)}, u32[]{:S(2)}) copy-start(f32[32,32]{1,0:T(8,128)} %constant.105.clone) | copy-start | bytes 12292
  25.4 27.8 %copy-start.6 = (f32[32,32]{1,0:T(8,128)S(1)}, f32[32,32]{1,0:T(8,128)}, u32[]{:S(2)}) copy-start(f32[32,32]{1,0:T(8,128)} %constant.104.clone) | copy-start | bytes 12292
  32.1 7.5 %collective-permute-start.1 = (f32[32,2048]{1,0:T(8,128)S(1)}, f32[32,2048]{1,0:T(8,128)S(1)}, u32[]{:S(2)}, u32[]{:S(2)}) collective-permute-start(f32[32,2048]{1,0:T(8,128)S(1)} %convolution_add_fusion.2), channel_id=1, source_target_pairs={{0,8},{4,12},{8,0},{12,4},{16,24},{20,28},{24,16},{28,20},{1,9},{5... | collective-permute-start | bytes 786440 | tf_op jit(solution)/shard_map/ppermute | solution.py:266
  40.0 13.2 %collective-permute-start.2 = (f32[32,2048]{1,0:T(8,128)S(1)}, f32[32,2048]{1,0:T(8,128)S(1)}, u32[]{:S(2)}, u32[]{:S(2)}) collective-permute-start(f32[32,2048]{1,0:T(8,128)S(1)} %convolution_add_fusion.1), channel_id=1, source_target_pairs={{0,16},{4,20},{8,24},{12,28},{16,0},{20,4},{24,8},{28,12},{1,17},{... | collective-permute-start | bytes 786440 | tf_op jit(solution)/shard_map/ppermute | solution.py:266
where the time goes:
time: 94.2 us; the launch traced here: 94 us
  Pallas kernels  40.7 us (43%)
  waiting for transfers between devices  20.7 us (22%)
  blocking collectives  14.1 us (15%)
  starting transfers between devices  7.51 us (8%)
  matrix products  6.66 us (7%)
  local copies, waits for them, and re-layouts  2.95 us (3%)
  other arithmetic  1.05 us (1%)
    pallas_call x1, Pallas kernels, eval_call(): pl.pallas_call(functools.partial(eval_kernel, blocks=blocks, leaves=leave...  25.2 us
    ppermute x3, waiting for transfers between devices, local(): partner = lax.ppermute(weights, 'leaf', route)  20.7 us
    pallas_call x1, Pallas kernels, leaf_call(): pl.pallas_call(functools.partial(leaf_kernel, digits=digits), grid=(digit...  15.5 us
    all_gather x2, blocking collectives, local(): lax.all_gather(weights[None, :, i * half:(i + 1) * half], 'blk', axis=0,...  14.1 us
    ppermute x3, starting transfers between devices, local(): partner = lax.ppermute(weights, 'leaf', route)  7.51 us
    dot_general x9, matrix products, mm(): return jnp.dot(a, b, precision=HIGHEST, preferred_element_type=jnp.float32)  6.66 us
  transfers between devices with their start and end apart: 3, of which 3 were waited for; matrix products, arithmetic and copies ran while one was open for 2% of the time, Pallas kernels for 0%

commit v1 on v0

--- a/solution.py
+++ b/solution.py
@@ -119,11 +119,21 @@
 
 
 def leaf_kernel(pos_ref, str_ref, mix_ref, out_ref, p_t, re_t, im_t, *, digits):
-    beta = pl.program_id(0)
-    rows = pl.ds(beta, LANES, stride=digits)
-    p_t[...] = pos_ref[rows, :].T
-    re_t[...] = str_ref[0, rows, :].T
-    im_t[...] = str_ref[1, rows, :].T
+    def tile(beta, carry):
+        rows = pl.ds(beta, LANES, stride=digits)
+        p_t[...] = pos_ref[rows, :].T
+        re_t[...] = str_ref[0, rows, :].T
+        im_t[...] = str_ref[1, rows, :].T
+        zero = jnp.zeros((8, LANES), jnp.float32)
+        acc = lax.fori_loop(0, PER_BOX // 8, chunk, tuple((zero, zero) for _ in range(R)), unroll=2)
+        low, high = list(acc[: R // 2]), list(acc[R // 2 :])
+        top = [high[0]]
+        for k in range(1, R // 2):
+            top.append(tuple(2.0 * h - m for h, m in zip(high[k], low[R // 2 - k])))
+        both = low + top
+        stack = jnp.concatenate([x for x, _ in both] + [y for _, y in both], axis=0)
+        out_ref[beta] = jnp.dot(mix_ref[...], stack, precision=HIGHEST, preferred_element_type=jnp.float32)
+        return carry
 
     def chunk(i, acc):
         here = pl.ds(pl.multiple_of(i * 8, 8), 8)
@@ -133,19 +143,18 @@
         a, b = re_t[here, :], im_t[here, :]
         v = r.astype(jnp.float32) * (2.0 / BOX_CELLS) - 1.0
         v2 = v + v
-        re0, im0 = c * a - s * b, s * a + c * b
-        re1, im1 = v * re0, v * im0
-        new = [(re0, im0), (re1, im1)]
-        for _ in range(2, R):
-            re0, re1 = re1, v2 * re1 - re0
-            im0, im1 = im1, v2 * im1 - im0
-            new.append((re1, im1))
-        return tuple((x + u, y + w) for (x, y), (u, w) in zip(acc, new))
-
-    zero = jnp.zeros((8, LANES), jnp.float32)
-    acc = lax.fori_loop(0, PER_BOX // 8, chunk, tuple((zero, zero) for _ in range(R)), unroll=2)
-    stack = jnp.concatenate([x for x, _ in acc] + [y for _, y in acc], axis=0)
-    out_ref[0] = jnp.dot(mix_ref[...], stack, precision=HIGHEST, preferred_element_type=jnp.float32)
+        cheb = [None, v]
+        for k in range(2, R // 2 + 1):
+            cheb.append(v2 * v - 1.0 if k == 2 else v2 * cheb[-1] - cheb[-2])
+        x, y = c * a - s * b, s * a + c * b
+        out = []
+        for part, (x, y) in enumerate([(x, y), (cheb[-1] * x, cheb[-1] * y)]):
+            for k in range(R // 2):
+                u, w = acc[part * (R // 2) + k]
+                out.append((u + x, w + y) if k == 0 else (u + cheb[k] * x, w + cheb[k] * y))
+        return tuple(out)
+
+    lax.fori_loop(0, digits, tile, 0)
 
 
 def leaf_call(pos, strengths):
@@ -154,10 +163,9 @@
     whole = pl.BlockSpec(memory_space=pltpu.VMEM)
     return pl.pallas_call(
         functools.partial(leaf_kernel, digits=digits),
-        grid=(digits,),
         out_shape=jax.ShapeDtypeStruct((digits, 2 * R, LANES), jnp.float32),
         in_specs=[whole, whole, whole],
-        out_specs=pl.BlockSpec((1, 2 * R, LANES), lambda b: (b, 0, 0)),
+        out_specs=whole,
         scratch_shapes=[
             pltpu.VMEM((LANES, LANES), jnp.int32),
             pltpu.VMEM((LANES, LANES), jnp.float32),
@@ -167,65 +175,164 @@
     )(pos, strengths, jnp.asarray(leaf_matrix()))
 
 
-def eval_kernel(suffix_ref, tgt_ref, co_ref, out_ref, g_t, re_t, im_t, *, blocks, leaves, depth, rows):
+MAGIC = 1.5 * 2.0**23
+
+
+def finish_kernel(w_ref, tgt_hbm, m_ref, out_hbm, tgt, out, bufs, got, coefs, g_t, re_t, im_t,
+                  send, recv, gsend, grecv, tsem, osem, *, leaves, blocks, chunks, depth, rows):
+    leaf_no, blk_no = lax.axis_index("leaf"), lax.axis_index("blk")
+    bits = leaves.bit_length() - 1
+    boxes = w_ref.shape[1]
+    width = boxes // chunks
+    tiles = width // LANES
     cells = BOX_CELLS * 2**depth
     ticks = TOP_TICKS // 2**depth
     half = R // 2
-    tile = pl.program_id(0)
-    lane = lax.broadcasted_iota(jnp.int32, (1, LANES), 1)
-    box = (tile * LANES + lane) * leaves + suffix_ref[0]
-    center = box * ticks + ticks // 2
-    g_t[...] = (tgt_ref[...].T - center).astype(jnp.float32)
+    sides = [leaf_no // 2**k % 2 for k in range(bits)]
+    partners = [leaf_no + (1 - 2 * sides[k]) * 2**k for k in range(bits)]
+    suffix = jnp.int32(0)
+    for k in range(bits):
+        suffix = 2 * suffix + sides[k]
+    peers = [lax.rem(blk_no + d, blocks) for d in range(1, blocks)]
+    fetch = pltpu.make_async_copy(tgt_hbm, tgt, tsem)
+    fetch.start()
+
+    barrier = pltpu.get_barrier_semaphore()
+    for k in range(bits):
+        pl.semaphore_signal(barrier, inc=1, device_id=(partners[k], blk_no), device_id_type=pl.DeviceIdType.MESH)
+    for peer in peers:
+        pl.semaphore_signal(barrier, inc=1, device_id=(leaf_no, peer), device_id_type=pl.DeviceIdType.MESH)
+    pl.semaphore_wait(barrier, bits + blocks - 1)
+
+    def own(stage, c):
+        return w_ref.at[:, pl.ds(c * width, width)] if stage == 0 else bufs.at[stage - 1, c]
+
+    def exchange(stage, c):
+        return pltpu.make_async_remote_copy(
+            src_ref=own(stage, c), dst_ref=got.at[stage, c],
+            send_sem=send.at[stage, c], recv_sem=recv.at[stage, c],
+            device_id=(partners[stage], blk_no), device_id_type=pl.DeviceIdType.MESH,
+        )
+
+    def spread(d, c):
+        here = coefs.at[blk_no, pl.ds(c * tiles, tiles)]
+        return pltpu.make_async_remote_copy(
+            src_ref=here, dst_ref=here,
+            send_sem=gsend.at[d - 1, c], recv_sem=grecv.at[d - 1, c],
+            device_id=(leaf_no, peers[d - 1]), device_id_type=pl.DeviceIdType.MESH,
+        )
+
+    def combine(stage, c):
+        exchange(stage, c).wait_recv()
+        m_own, m_other = m_ref[stage, sides[stage], 0], m_ref[stage, sides[stage], 1]
+        w = mm(m_own, own(stage, c)[...]) + mm(m_other, got[stage, c])
+        if stage < bits - 1:
+            bufs[stage, c] = w
+            exchange(stage + 1, c).start()
+        else:
+            for i in range(tiles):
+                coefs[blk_no, c * tiles + i] = w[:, i * LANES : (i + 1) * LANES]
+            for d in range(1, blocks):
+                spread(d, c).start()
+
     offsets = 2 * node_offsets(cells) - cells + 1
 
     def turned(g, factor):
         y = g * factor
         if abs(factor) * (ticks // 2) > 0.5:
-            y = y - jnp.round(y)
+            y = y - ((y + MAGIC) - MAGIC)
         return cos_sin_turns(y)
 
-    def chunk(i, carry):
-        here = pl.ds(pl.multiple_of(i * rows, rows), rows)
-        g = g_t[here, :]
-        acc = [[None, None] for _ in range(blocks)]
-        for t in range(half):
-            c, s = turned(g, float(offsets[t]) * 2.0**-33)
-            for q in range(blocks):
-                for part in range(2):
-                    sc = co_ref[q, pl.ds(part * half + t, 1), :]
-                    sd = co_ref[q, pl.ds((2 + part) * half + t, 1), :]
-                    term = sc * c + sd * s
-                    acc[q][part] = term if t == 0 else acc[q][part] + term
-        zc, zs = turned(g, float(cells) * 2.0**-32)
-        re, im = acc[blocks - 1]
-        for q in range(blocks - 2, -1, -1):
-            re, im = zc * re - zs * im + acc[q][0], zc * im + zs * re + acc[q][1]
-        pc, ps = turned(g, float(cells - 1) * 2.0**-33)
-        re_t[here, :] = pc * re - ps * im
-        im_t[here, :] = pc * im + ps * re
+    lane = lax.broadcasted_iota(jnp.int32, (1, LANES), 1)
+
+    def evaluate(tile, carry):
+        box = (tile * LANES + lane) * leaves + suffix
+        center = box * ticks + ticks // 2
+        first = pl.multiple_of(tile * LANES, LANES)
+        g_t[...] = (tgt[pl.ds(first, LANES), :].T - center).astype(jnp.float32)
+
+        def chunk(i, carry):
+            here = pl.ds(pl.multiple_of(i * rows, rows), rows)
+            g = g_t[here, :]
+            acc = [[None, None] for _ in range(blocks)]
+            for t in range(half):
+                c, s = turned(g, float(offsets[t]) * 2.0**-33)
+                for q in range(blocks):
+                    for part in range(2):
+                        sc = coefs[q, tile, pl.ds(part * half + t, 1), :]
+                        sd = coefs[q, tile, pl.ds((2 + part) * half + t, 1), :]
+                        term = sc * c + sd * s
+                        acc[q][part] = term if t == 0 else acc[q][part] + term
+            zc, zs = turned(g, float(cells) * 2.0**-32)
+            re, im = acc[blocks - 1]
+            for q in range(blocks - 2, -1, -1):
+                re, im = zc * re - zs * im + acc[q][0], zc * im + zs * re + acc[q][1]
+            pc, ps = turned(g, float(cells - 1) * 2.0**-33)
+            re_t[here, :] = pc * re - ps * im
+            im_t[here, :] = pc * im + ps * re
+            return carry
+
+        lax.fori_loop(0, TGT_BOX // rows, chunk, 0)
+        out[pl.ds(2 * first, LANES, stride=2), :] = re_t[...].T
+        out[pl.ds(2 * first + 1, LANES, stride=2), :] = im_t[...].T
         return carry
 
-    lax.fori_loop(0, TGT_BOX // rows, chunk, 0)
-    out_ref[pl.ds(0, LANES, stride=2), :] = re_t[...].T
-    out_ref[pl.ds(1, LANES, stride=2), :] = im_t[...].T
-
-
-def eval_call(suffix, ticks, coefs, leaves, depth):
+    def put(c):
+        span = pl.ds(2 * c * width, 2 * width)
+        return pltpu.make_async_copy(out.at[span], out_hbm.at[span], osem.at[c])
+
+    def field(c):
+        if c == 0:
+            fetch.wait()
+        for d in range(1, blocks):
+            spread(d, c).wait_recv()
+        lax.fori_loop(c * tiles, (c + 1) * tiles, evaluate, 0)
+        put(c).start()
+
+    for c in range(chunks):
+        exchange(0, c).start()
+    for step in range(chunks + bits - 2):
+        for stage in range(bits - 1, -1, -1):
+            if 0 <= step - stage < chunks:
+                combine(stage, step - stage)
+    field(0)
+    combine(bits - 1, chunks - 1)
+    for c in range(1, chunks):
+        field(c)
+    for c in range(chunks):
+        for stage in range(bits):
+            exchange(stage, c).wait_send()
+        for d in range(1, blocks):
+            spread(d, c).wait_send()
+        put(c).wait()
+
+
+def finish_call(weights, ticks, matrices, leaves, blocks, depth, chunks):
     boxes = ticks.shape[0]
-    blocks = coefs.shape[0]
+    bits = leaves.bit_length() - 1
+    width = boxes // chunks
+    whole = pl.BlockSpec(memory_space=pltpu.VMEM)
+    anywhere = pl.BlockSpec(memory_space=pl.ANY)
+    dma = pltpu.SemaphoreType.DMA
     return pl.pallas_call(
-        functools.partial(eval_kernel, blocks=blocks, leaves=leaves, depth=depth, rows=16),
-        grid=(boxes // LANES,),
+        functools.partial(finish_kernel, leaves=leaves, blocks=blocks, chunks=chunks, depth=depth, rows=16),
         out_shape=jax.ShapeDtypeStruct((2 * boxes, TGT_BOX), jnp.float32),
-        in_specs=[
-            pl.BlockSpec(memory_space=pltpu.SMEM),
-            pl.BlockSpec((LANES, TGT_BOX), lambda i: (i, 0)),
-            pl.BlockSpec((blocks, 2 * R, LANES), lambda i: (0, 0, i)),
+        in_specs=[whole, anywhere, whole],
+        out_specs=anywhere,
+        scratch_shapes=[
+            pltpu.VMEM((boxes, TGT_BOX), jnp.int32),
+            pltpu.VMEM((2 * boxes, TGT_BOX), jnp.float32),
+            pltpu.VMEM((bits - 1, chunks, 2 * R, width), jnp.float32),
+            pltpu.VMEM((bits, chunks, 2 * R, width), jnp.float32),
+            pltpu.VMEM((blocks, boxes // LANES, 2 * R, LANES), jnp.float32),
+        ] + [pltpu.VMEM((TGT_BOX, LANES), jnp.float32)] * 3 + [
+            dma((bits, chunks)), dma((bits, chunks)),
+            dma((blocks - 1, chunks)), dma((blocks - 1, chunks)),
+            dma, dma((chunks,)),
         ],
-        out_specs=pl.BlockSpec((2 * LANES, TGT_BOX), lambda i: (i, 0)),
-        scratch_shapes=[pltpu.VMEM((TGT_BOX, LANES), jnp.float32)] * 3,
-        name="evaluate",
-    )(suffix.reshape(1), ticks, coefs)
+        compiler_params=pltpu.CompilerParams(collective_id=0, has_side_effects=True),
+        name="finish",
+    )(weights, ticks, matrices)
 
 
 def table(m):
@@ -254,27 +361,17 @@
 def local(src_pos, strengths, tgt_pos):
     leaf_count = lax.axis_size("leaf")
     leaf_bits = leaf_count.bit_length() - 1
-    leaf_no = lax.axis_index("leaf")
     boxes = src_pos.shape[1] // PER_BOX
     local_depth = boxes.bit_length() - 1
     leaf = leaf_call(src_pos.reshape(boxes, PER_BOX), strengths.reshape(2, boxes, PER_BOX))
     weights = local_tree(leaf, boxes)
-    suffix = jnp.int32(0)
-    for bit_no in range(leaf_bits):
-        side = leaf_no // 2**bit_no % 2
-        route = [(k, k ^ (1 << bit_no)) for k in range(leaf_count)]
-        partner = lax.ppermute(weights, "leaf", route)
-        m = step_matrix(local_depth + bit_no)
-        if bit_no == leaf_bits - 1:
-            m = np.einsum("xy,ejyz->ejxz", fold_pairs(), m)
-        own = jnp.where(side == 0, table(m[0, 0]), table(m[1, 1]))
-        other = jnp.where(side == 0, table(m[0, 1]), table(m[1, 0]))
-        weights = mm(own, weights) + mm(other, partner)
-        suffix = 2 * suffix + side
-    half = boxes // 2
-    parts = [lax.all_gather(weights[None, :, i * half : (i + 1) * half], "blk", axis=0, tiled=True) for i in range(2)]
-    coefs = jnp.concatenate(parts, axis=2)
-    out = eval_call(suffix, tgt_pos.reshape(boxes, TGT_BOX), coefs, leaf_count, local_depth + leaf_bits)
+    steps = np.stack([step_matrix(local_depth + k) for k in range(leaf_bits)])
+    steps[-1] = np.einsum("xy,ejyz->ejxz", fold_pairs(), steps[-1])
+    steps[:, 1] = steps[:, 1, ::-1]
+    out = finish_call(
+        weights, tgt_pos.reshape(boxes, TGT_BOX), table(steps), leaf_count, lax.axis_size("blk"),
+        local_depth + leaf_bits, 4,
+    )
     return out.reshape(boxes, 2, TGT_BOX).transpose(1, 0, 2).reshape(2, boxes * TGT_BOX)
 
 

time: 94.2 us -> 80.5 us (0.85)
  Pallas kernels: 40.7 us -> 70.2 us
  waiting for transfers between devices: 20.7 us -> 0 us
  blocking collectives: 14.1 us -> 0 us
  starting transfers between devices: 7.51 us -> 0 us
  local copies, waits for them, and re-layouts: 2.95 us -> 6.18 us
  matrix products: 6.66 us -> 3.76 us
  other arithmetic: 1.05 us -> 0 us
    pallas_call x2, Pallas kernels: 40.7 us -> 70.2 us  [the longest x1 55.8 us: finish_call(): pl.pallas_call(functools.partial(finish_kernel, leaves=leaves, blocks=blo...]
    ppermute x3 -> x0, waiting for transfers between devices: 20.7 us -> none  [local(): partner = lax.ppermute(weights, 'leaf', route)]
    all_gather x2 -> x0, blocking collectives: 14.1 us -> none  [local(): lax.all_gather(weights[None, :, i * half:(i + 1) * half], 'blk', axis=0,...]
    ppermute x3 -> x0, starting transfers between devices: 7.51 us -> none  [local(): partner = lax.ppermute(weights, 'leaf', route)]
    dot_general x9 -> x3, matrix products: 6.66 us -> 3.76 us  [mm(): return jnp.dot(a, b, precision=HIGHEST, preferred_element_type=jnp.float32)]
    unnamed x30 -> x7, local copies, waits for them, and re-layouts: 0.25 us -> 2.79 us
    concatenate x1 -> x0, other arithmetic: 1.05 us -> none  [local(): coefs = jnp.concatenate(parts, axis=2)]
  transfers between devices with their start and end apart: 3 -> 0, of which waited for: 3 -> 0; matrix products, arithmetic and copies ran while one was open for 2% -> 0% of each run, Pallas kernels for 0% -> 0%
where the time goes in v1:
time: 80.5 us; the launch traced here: 80.2 us
  Pallas kernels  70.2 us (87%)
  local copies, waits for them, and re-layouts  6.18 us (8%)
  matrix products  3.76 us (5%)
    pallas_call x1, Pallas kernels, finish_call(): pl.pallas_call(functools.partial(finish_kernel, leaves=leaves, blocks=blo...  55.8 us
    pallas_call x1, Pallas kernels, leaf_call(): pl.pallas_call(functools.partial(leaf_kernel, digits=digits), out_shape=j...  14.4 us
    dot_general x3, matrix products, mm(): return jnp.dot(a, b, precision=HIGHEST, preferred_element_type=jnp.float32)  3.76 us
    unnamed x7, local copies, waits for them, and re-layouts  2.79 us

profile of v1, /device:TPU:0, one launch (start us, length us, event | category | flops | bytes accessed | tf_op | source)
XLA Modules:
  0.0 80.2 jit_solution(6165253853311160435)
XLA Ops:
  0.0 0.0 copy-start.1
  0.0 14.4 %leaf.1 = f32[16,32,128]{2,1,0:T(8,128)} custom-call(s32[2048,128]{1,0:T(8,128)} %bitcast.40, f32[2,2048,128]{2,1,0:T(8,128)} %bitcast.37, f32[32,256]{1,0:T(8,128)} %constant.10.clone.mix_ref), custom_call_target="tpu_custom_call" | custom-call | tf_op jit(solution)/shard_map/leaf/pallas_call | solution.py:164
  14.4 0.0 copy-done.1
  14.4 2.2 %fusion = f32[512,128]{0,1:T(8,128)S(1)} fusion(f32[512,512]{1,0:T(8,128)S(1)} %copy-done.1, f32[512,128]{1,0:T(8,128)} %bitcast.41), kind=kOutput, calls=%fused_computation | convolution fusion | flops 402653184 | bytes 1572864 | tf_op jit(solution)/shard_map/dot_general | solution.py:343
  16.6 0.0 copy-start
  16.6 0.3 reshape.39
  16.8 0.3 copy.12
  17.2 0.4 reshape.40
  17.6 0.2 copy-done
  17.8 1.2 %fusion.1 = f32[512,128]{0,1:T(8,128)S(1)} fusion(f32[512,512]{1,0:T(8,128)S(1)} %copy-done, f32[512,128]{0,1:T(8,128)S(1)} %reshape.40), kind=kOutput, calls=%fused_computation.1 | convolution fusion | flops 402653184 | bytes 1572864 | tf_op jit(solution)/shard_map/dot_general | solution.py:343
  19.0 0.0 copy-start.2
  19.0 0.3 reshape.41
  19.3 0.3 copy.14
  19.6 0.3 reshape.42
  19.9 0.0 copy-done.2
  20.0 0.4 fusion.2
  20.4 0.4 copy.15
  20.8 1.0 %copy.16.w_ref = f32[32,2048]{1,0:T(8,128)} copy(f32[32,2048]{0,1:T(8,128)S(1)} %bitcast.34) | data formatting | bytes 524288 | tf_op jit(solution)/shard_map/reshape | solution.py:358
  21.8 55.8 %finish.1 = f32[4096,128]{1,0:T(8,128)} custom-call(f32[32,2048]{1,0:T(8,128)} %copy.16.w_ref, s32[2048,128]{1,0:T(8,128)} %bitcast.38, f32[3,2,2,32,32]{4,3,2,1,0:T(8,128)} %constant.14.clone.m_ref), custom_call_target="tpu_custom_call" | custom-call | tf_op jit(solution)/shard_map/finish/pallas_call | solution.py:317
  77.6 2.6 %copy.21 = f32[2,262144]{1,0:T(2,128)} copy(f32[2,262144]{1,0:T(2,128)} %bitcast.33) | data formatting | bytes 4194304
Async XLA Ops:
  0.0 14.4 %copy-start.1 = (f32[512,512]{1,0:T(8,128)S(1)}, f32[512,512]{1,0:T(8,128)}, u32[]{:S(2)}) copy-start(f32[512,512]{1,0:T(8,128)} %constant.11.clone) | copy-start | bytes 3145732
  16.6 1.2 %copy-start = (f32[512,512]{1,0:T(8,128)S(1)}, f32[512,512]{1,0:T(8,128)}, u32[]{:S(2)}) copy-start(f32[512,512]{1,0:T(8,128)} %constant.12.clone) | copy-start | bytes 3145732
  19.0 1.0 %copy-start.2 = (f32[256,256]{1,0:T(8,128)S(1)}, f32[256,256]{1,0:T(8,128)}, u32[]{:S(2)}) copy-start(f32[256,256]{1,0:T(8,128)} %constant.13.clone) | copy-start | bytes 786436

commit v2 on v1

--- a/solution.py
+++ b/solution.py
@@ -24,8 +24,8 @@
     return [float(c) for c in cheb.convert(kind=np.polynomial.Polynomial).coef]
 
 
-COS_POLY = fit_even(lambda y: np.cos(2 * np.pi * y), 0.5, 6)
-SIN_POLY = fit_even(lambda y: np.sin(2 * np.pi * y) / y, 0.5, 6)
+COS_POLY = fit_even(lambda y: np.cos(np.pi * y), 0.5, 5)
+SIN_POLY = fit_even(lambda y: np.sin(np.pi * y) / y, 0.5, 4)
 
 
 def horner(coefs, u):
@@ -37,7 +37,9 @@
 
 def cos_sin_turns(y):
     u = y * y
-    return horner(COS_POLY, u), y * horner(SIN_POLY, u)
+    c, s = horner(COS_POLY, u), y * horner(SIN_POLY, u)
+    twice = s + s
+    return 1.0 - twice * s, twice * c
 
 
 def node_offsets(box_cells):
@@ -119,13 +121,19 @@
 
 
 def leaf_kernel(pos_ref, str_ref, mix_ref, out_ref, p_t, re_t, im_t, *, digits):
+    def turn_over(beta, slot):
+        rows = pl.ds(beta, LANES, stride=digits)
+        p_t[slot] = pos_ref[rows, :].T
+        re_t[slot] = str_ref[0, rows, :].T
+        im_t[slot] = str_ref[1, rows, :].T
+
     def tile(beta, carry):
-        rows = pl.ds(beta, LANES, stride=digits)
-        p_t[...] = pos_ref[rows, :].T
-        re_t[...] = str_ref[0, rows, :].T
-        im_t[...] = str_ref[1, rows, :].T
+        slot = lax.rem(beta, 2)
+        turn_over(jnp.minimum(beta + 1, digits - 1), 1 - slot)
         zero = jnp.zeros((8, LANES), jnp.float32)
-        acc = lax.fori_loop(0, PER_BOX // 8, chunk, tuple((zero, zero) for _ in range(R)), unroll=2)
+        acc = tuple((zero, zero) for _ in range(R))
+        for i in range(PER_BOX // 8):
+            acc = chunk(slot, i, acc)
         low, high = list(acc[: R // 2]), list(acc[R // 2 :])
         top = [high[0]]
         for k in range(1, R // 2):
@@ -135,12 +143,12 @@
         out_ref[beta] = jnp.dot(mix_ref[...], stack, precision=HIGHEST, preferred_element_type=jnp.float32)
         return carry
 
-    def chunk(i, acc):
-        here = pl.ds(pl.multiple_of(i * 8, 8), 8)
-        r = p_t[here, :] & (BOX_CELLS - 1)
+    def chunk(slot, i, acc):
+        here = pl.ds(i * 8, 8)
+        r = p_t[slot, here, :] & (BOX_CELLS - 1)
         turn = (r * (TOP_TICKS // 2)).astype(jnp.float32) * (2.0**-32)
         c, s = cos_sin_turns(turn)
-        a, b = re_t[here, :], im_t[here, :]
+        a, b = re_t[slot, here, :], im_t[slot, here, :]
         v = r.astype(jnp.float32) * (2.0 / BOX_CELLS) - 1.0
         v2 = v + v
         cheb = [None, v]
@@ -154,6 +162,7 @@
                 out.append((u + x, w + y) if k == 0 else (u + cheb[k] * x, w + cheb[k] * y))
         return tuple(out)
 
+    turn_over(0, 0)
     lax.fori_loop(0, digits, tile, 0)
 
 
@@ -167,9 +176,9 @@
         in_specs=[whole, whole, whole],
         out_specs=whole,
         scratch_shapes=[
-            pltpu.VMEM((LANES, LANES), jnp.int32),
-            pltpu.VMEM((LANES, LANES), jnp.float32),
-            pltpu.VMEM((LANES, LANES), jnp.float32),
+            pltpu.VMEM((2, LANES, LANES), jnp.int32),
+            pltpu.VMEM((2, LANES, LANES), jnp.float32),
+            pltpu.VMEM((2, LANES, LANES), jnp.float32),
         ],
         name="leaf",
     )(pos, strengths, jnp.asarray(leaf_matrix()))
@@ -289,16 +298,17 @@
         lax.fori_loop(c * tiles, (c + 1) * tiles, evaluate, 0)
         put(c).start()
 
-    for c in range(chunks):
+    ahead = min(3, chunks)
+    for c in range(ahead):
         exchange(0, c).start()
-    for step in range(chunks + bits - 2):
+    for step in range(chunks + bits):
         for stage in range(bits - 1, -1, -1):
             if 0 <= step - stage < chunks:
                 combine(stage, step - stage)
-    field(0)
-    combine(bits - 1, chunks - 1)
-    for c in range(1, chunks):
-        field(c)
+        if step + ahead < chunks:
+            exchange(0, step + ahead).start()
+        if step >= bits:
+            field(step - bits)
     for c in range(chunks):
         for stage in range(bits):
             exchange(stage, c).wait_send()
@@ -370,7 +380,7 @@
     steps[:, 1] = steps[:, 1, ::-1]
     out = finish_call(
         weights, tgt_pos.reshape(boxes, TGT_BOX), table(steps), leaf_count, lax.axis_size("blk"),
-        local_depth + leaf_bits, 4,
+        local_depth + leaf_bits, 8,
     )
     return out.reshape(boxes, 2, TGT_BOX).transpose(1, 0, 2).reshape(2, boxes * TGT_BOX)
 

time: 80.5 us -> 74.9 us (0.930)
  Pallas kernels: 70.2 us -> 64.6 us
    pallas_call x1, Pallas kernels: 55.8 us -> 52.5 us  [finish_call(): pl.pallas_call(functools.partial(finish_kernel, leaves=leaves, blocks=blo...]
    pallas_call x1, Pallas kernels: 14.4 us -> 12.1 us  [leaf_call(): pl.pallas_call(functools.partial(leaf_kernel, digits=digits), out_shape=j...]
where the time goes in v2:
time: 74.9 us; the launch traced here: 74.6 us
  Pallas kernels  64.6 us (86%)
  local copies, waits for them, and re-layouts  6.18 us (8%)
  matrix products  3.76 us (5%)
    pallas_call x1, Pallas kernels, finish_call(): pl.pallas_call(functools.partial(finish_kernel, leaves=leaves, blocks=blo...  52.5 us
    pallas_call x1, Pallas kernels, leaf_call(): pl.pallas_call(functools.partial(leaf_kernel, digits=digits), out_shape=j...  12.1 us
    dot_general x3, matrix products, mm(): return jnp.dot(a, b, precision=HIGHEST, preferred_element_type=jnp.float32)  3.76 us
    unnamed x7, local copies, waits for them, and re-layouts  2.79 us

profile of v2, /device:TPU:0, one launch (start us, length us, event | category | flops | bytes accessed | tf_op | source)
XLA Modules:
  0.0 74.6 jit_solution(9111570043611345490)
XLA Ops:
  0.0 0.0 copy-start.1
  0.0 12.1 %leaf.1 = f32[16,32,128]{2,1,0:T(8,128)} custom-call(s32[2048,128]{1,0:T(8,128)} %bitcast.40, f32[2,2048,128]{2,1,0:T(8,128)} %bitcast.37, f32[32,256]{1,0:T(8,128)} %constant.10.clone.mix_ref), custom_call_target="tpu_custom_call" | custom-call | tf_op jit(solution)/shard_map/leaf/pallas_call | solution.py:173
  12.1 0.0 copy-done.1
  12.1 2.1 %fusion = f32[512,128]{0,1:T(8,128)S(1)} fusion(f32[512,512]{1,0:T(8,128)S(1)} %copy-done.1, f32[512,128]{1,0:T(8,128)} %bitcast.41), kind=kOutput, calls=%fused_computation | convolution fusion | flops 402653184 | bytes 1572864 | tf_op jit(solution)/shard_map/dot_general | solution.py:353
  14.2 0.0 copy-start
  14.3 0.3 reshape.39
  14.5 0.3 copy.12
  14.9 0.4 reshape.40
  15.3 0.2 copy-done
  15.5 1.2 %fusion.1 = f32[512,128]{0,1:T(8,128)S(1)} fusion(f32[512,512]{1,0:T(8,128)S(1)} %copy-done, f32[512,128]{0,1:T(8,128)S(1)} %reshape.40), kind=kOutput, calls=%fused_computation.1 | convolution fusion | flops 402653184 | bytes 1572864 | tf_op jit(solution)/shard_map/dot_general | solution.py:353
  16.7 0.0 copy-start.2
  16.7 0.3 reshape.41
  17.0 0.3 copy.14
  17.3 0.3 reshape.42
  17.6 0.0 copy-done.2
  17.6 0.4 fusion.2
  18.1 0.4 copy.15
  18.5 1.0 %copy.16.w_ref = f32[32,2048]{1,0:T(8,128)} copy(f32[32,2048]{0,1:T(8,128)S(1)} %bitcast.34) | data formatting | bytes 524288 | tf_op jit(solution)/shard_map/reshape | solution.py:368
  19.5 52.5 %finish.1 = f32[4096,128]{1,0:T(8,128)} custom-call(f32[32,2048]{1,0:T(8,128)} %copy.16.w_ref, s32[2048,128]{1,0:T(8,128)} %bitcast.38, f32[3,2,2,32,32]{4,3,2,1,0:T(8,128)} %constant.14.clone.m_ref), custom_call_target="tpu_custom_call" | custom-call | tf_op jit(solution)/shard_map/finish/pallas_call | solution.py:327
  72.0 2.6 %copy.21 = f32[2,262144]{1,0:T(2,128)} copy(f32[2,262144]{1,0:T(2,128)} %bitcast.33) | data formatting | bytes 4194304
Async XLA Ops:
  0.0 12.1 %copy-start.1 = (f32[512,512]{1,0:T(8,128)S(1)}, f32[512,512]{1,0:T(8,128)}, u32[]{:S(2)}) copy-start(f32[512,512]{1,0:T(8,128)} %constant.11.clone) | copy-start | bytes 3145732
  14.2 1.2 %copy-start = (f32[512,512]{1,0:T(8,128)S(1)}, f32[512,512]{1,0:T(8,128)}, u32[]{:S(2)}) copy-start(f32[512,512]{1,0:T(8,128)} %constant.12.clone) | copy-start | bytes 3145732
  16.7 1.0 %copy-start.2 = (f32[256,256]{1,0:T(8,128)S(1)}, f32[256,256]{1,0:T(8,128)}, u32[]{:S(2)}) copy-start(f32[256,256]{1,0:T(8,128)} %constant.13.clone) | copy-start | bytes 786436

commit v3 on v2

--- a/solution.py
+++ b/solution.py
@@ -231,18 +231,25 @@
             device_id=(leaf_no, peers[d - 1]), device_id_type=pl.DeviceIdType.MESH,
         )
 
-    def combine(stage, c):
-        exchange(stage, c).wait_recv()
-        m_own, m_other = m_ref[stage, sides[stage], 0], m_ref[stage, sides[stage], 1]
-        w = mm(m_own, own(stage, c)[...]) + mm(m_other, got[stage, c])
-        if stage < bits - 1:
-            bufs[stage, c] = w
-            exchange(stage + 1, c).start()
-        else:
-            for i in range(tiles):
-                coefs[blk_no, c * tiles + i] = w[:, i * LANES : (i + 1) * LANES]
-            for d in range(1, blocks):
-                spread(d, c).start()
+    def combine(todo):
+        for stage, c in todo:
+            exchange(stage, c).wait_recv()
+        results = []
+        for stage, c in todo:
+            pair = jnp.concatenate([own(stage, c)[...], got[stage, c]], axis=0)
+            results.append(mm(m_ref[stage, sides[stage]], pair))
+        for (stage, c), w in zip(todo, results):
+            if stage < bits - 1:
+                bufs[stage, c] = w
+            else:
+                for i in range(tiles):
+                    coefs[blk_no, c * tiles + i] = w[:, i * LANES : (i + 1) * LANES]
+        for stage, c in todo:
+            if stage < bits - 1:
+                exchange(stage + 1, c).start()
+            else:
+                for d in range(1, blocks):
+                    spread(d, c).start()
 
     offsets = 2 * node_offsets(cells) - cells + 1
 
@@ -302,9 +309,7 @@
     for c in range(ahead):
         exchange(0, c).start()
     for step in range(chunks + bits):
-        for stage in range(bits - 1, -1, -1):
-            if 0 <= step - stage < chunks:
-                combine(stage, step - stage)
+        combine([(k, step - k) for k in range(bits - 1, -1, -1) if 0 <= step - k < chunks])
         if step + ahead < chunks:
             exchange(0, step + ahead).start()
         if step >= bits:
@@ -378,6 +383,7 @@
     steps = np.stack([step_matrix(local_depth + k) for k in range(leaf_bits)])
     steps[-1] = np.einsum("xy,ejyz->ejxz", fold_pairs(), steps[-1])
     steps[:, 1] = steps[:, 1, ::-1]
+    steps = np.concatenate([steps[:, :, 0], steps[:, :, 1]], axis=-1)
     out = finish_call(
         weights, tgt_pos.reshape(boxes, TGT_BOX), table(steps), leaf_count, lax.axis_size("blk"),
         local_depth + leaf_bits, 8,

time: 74.9 us -> 72.4 us (0.967)
  Pallas kernels: 64.6 us -> 62.1 us
    pallas_call x1, Pallas kernels: 52.5 us -> 50 us  [finish_call(): pl.pallas_call(functools.partial(finish_kernel, leaves=leaves, blocks=blo...]
where the time goes in v3:
time: 72.4 us; the launch traced here: 72.2 us
  Pallas kernels  62.1 us (86%)
  local copies, waits for them, and re-layouts  6.18 us (9%)
  matrix products  3.76 us (5%)
    pallas_call x1, Pallas kernels, finish_call(): pl.pallas_call(functools.partial(finish_kernel, leaves=leaves, blocks=blo...  50 us
    pallas_call x1, Pallas kernels, leaf_call(): pl.pallas_call(functools.partial(leaf_kernel, digits=digits), out_shape=j...  12.1 us
    dot_general x3, matrix products, mm(): return jnp.dot(a, b, precision=HIGHEST, preferred_element_type=jnp.float32)  3.76 us
    unnamed x7, local copies, waits for them, and re-layouts  2.79 us

profile of v3, /device:TPU:0, one launch (start us, length us, event | category | flops | bytes accessed | tf_op | source)
XLA Modules:
  0.0 72.2 jit_solution(17958447787370234072)
XLA Ops:
  0.0 0.0 copy-start.1
  0.0 12.1 %leaf.1 = f32[16,32,128]{2,1,0:T(8,128)} custom-call(s32[2048,128]{1,0:T(8,128)} %bitcast.39, f32[2,2048,128]{2,1,0:T(8,128)} %bitcast.37, f32[32,256]{1,0:T(8,128)} %constant.10.clone.mix_ref), custom_call_target="tpu_custom_call" | custom-call | tf_op jit(solution)/shard_map/leaf/pallas_call | solution.py:173
  12.1 0.0 copy-done.1
  12.1 2.1 %fusion = f32[512,128]{0,1:T(8,128)S(1)} fusion(f32[512,512]{1,0:T(8,128)S(1)} %copy-done.1, f32[512,128]{1,0:T(8,128)} %bitcast.41), kind=kOutput, calls=%fused_computation | convolution fusion | flops 402653184 | bytes 1572864 | tf_op jit(solution)/shard_map/dot_general | solution.py:358
  14.2 0.0 copy-start
  14.3 0.3 reshape.39
  14.5 0.3 copy.12
  14.9 0.4 reshape.40
  15.3 0.2 copy-done
  15.5 1.2 %fusion.1 = f32[512,128]{0,1:T(8,128)S(1)} fusion(f32[512,512]{1,0:T(8,128)S(1)} %copy-done, f32[512,128]{0,1:T(8,128)S(1)} %reshape.40), kind=kOutput, calls=%fused_computation.1 | convolution fusion | flops 402653184 | bytes 1572864 | tf_op jit(solution)/shard_map/dot_general | solution.py:358
  16.7 0.0 copy-start.2
  16.7 0.3 reshape.41
  17.0 0.3 copy.14
  17.3 0.3 reshape.42
  17.6 0.0 copy-done.2
  17.6 0.4 fusion.2
  18.1 0.4 copy.15
  18.5 1.0 %copy.16.w_ref = f32[32,2048]{1,0:T(8,128)} copy(f32[32,2048]{0,1:T(8,128)S(1)} %bitcast.34) | data formatting | bytes 524288 | tf_op jit(solution)/shard_map/reshape | solution.py:373
  19.5 50.0 %finish.1 = f32[4096,128]{1,0:T(8,128)} custom-call(f32[32,2048]{1,0:T(8,128)} %copy.16.w_ref, s32[2048,128]{1,0:T(8,128)} %bitcast.40, f32[3,2,32,64]{3,2,1,0:T(8,128)} %constant.14.clone.m_ref), custom_call_target="tpu_custom_call" | custom-call | tf_op jit(solution)/shard_map/finish/pallas_call | solution.py:332
  69.5 2.6 %copy.21 = f32[2,262144]{1,0:T(2,128)} copy(f32[2,262144]{1,0:T(2,128)} %bitcast.33) | data formatting | bytes 4194304
Async XLA Ops:
  0.0 12.1 %copy-start.1 = (f32[512,512]{1,0:T(8,128)S(1)}, f32[512,512]{1,0:T(8,128)}, u32[]{:S(2)}) copy-start(f32[512,512]{1,0:T(8,128)} %constant.11.clone) | copy-start | bytes 3145732
  14.2 1.2 %copy-start = (f32[512,512]{1,0:T(8,128)S(1)}, f32[512,512]{1,0:T(8,128)}, u32[]{:S(2)}) copy-start(f32[512,512]{1,0:T(8,128)} %constant.12.clone) | copy-start | bytes 3145732
  16.7 1.0 %copy-start.2 = (f32[256,256]{1,0:T(8,128)S(1)}, f32[256,256]{1,0:T(8,128)}, u32[]{:S(2)}) copy-start(f32[256,256]{1,0:T(8,128)} %constant.13.clone) | copy-start | bytes 786436
